TPU v7x, 32 devices: a whole 2x2x4 slice. The times are simulated.
32 devices in a mesh: group: 4 (over z), seq: 4 (over y, core), mp: 2 (over x).
Axes of the slice: x: 2, y: 2, z: 4, core: 2. Of those that a mesh axis runs over, the one named last changes fastest.
Arguments:
- patches: bfloat16 [8192, 640], P(('group', 'seq')), may hold values from -6 to 6
- w_merge1: bfloat16 [4, 640, 2560], P(None, 'seq', 'mp'), may hold values from -0.125 to 0.125
- w_merge2: bfloat16 [2560, 4096], P('mp', 'seq'), may hold values from -0.125 to 0.125
- w_query: bfloat16 [4096, 4096], P('seq', 'mp'), may hold values from -0.09375 to 0.09375
- w_keyval: bfloat16 [4096, 2, 1024], P('seq', None, 'mp'), may hold values from -0.09375 to 0.09375
- attn_grad: bfloat16 [2048, 4096], P(('group', 'seq'), 'mp'), may hold values from -6 to 6
- sample_ids: int32 [4, 512], P('group'), may hold values from 0 to 7, never falling along the last dimension, each value on 1 to 384 neighbouring positions
Outputs:
- patch_grad: bfloat16 [8192, 640], P(('group', 'seq', 'mp'))
Inputs may be any that keep to these rules, and one draw needn't show every extreme that they name: `sample_ids`: in each sequence never falls; every sample spans 1 to 384 tokens.
All inputs are finite; a program needn't handle non-finite values.
Results may differ from a plain program's by a relative error of at most 0.035.
Values may be sent and summed in bfloat16 or wider, within the bound.
No kernel may reach another device: no remote copies, remote signals or barrier semaphores. Data moves between devices by JAX's collectives and lax.ppermute only.
A program may use at most 128 MiB of HBM per device.

v0:
```python
import jax
import jax.numpy as jnp
from jax import lax
from jax.sharding import PartitionSpec as P

HEAD = 128


EPSILON = 1e-06
NEGATIVE = 1e30


def shifted_2(value, axis, steps):
    count = lax.axis_size(axis)
    initial, last = (max(0, -steps), min(count, count - steps))
    return lax.ppermute(value, axis, [(source, source + steps) for source in range(initial, last)])


def gelu_grad(inputs):
    normal_cdf = 0.5 * (1.0 + lax.erf(inputs * 0.7071067811865476))
    normal_pdf = jnp.exp(-0.5 * inputs * inputs) * 0.3989422804014327
    return normal_cdf + inputs * normal_pdf


def fetch_earlier(own_keyval, offset):
    return shifted_2(own_keyval, "seq", offset)


def return_terms(terms, offset):
    return (
        shifted_2(terms[0].astype(jnp.bfloat16), "seq", -offset).astype(jnp.float32),
        shifted_2(terms[1].astype(jnp.bfloat16), "seq", -offset).astype(jnp.float32),
    )


def local(patches, w_merge1, w_merge2, w_query, w_keyval, attn_grad, sample_ids):
    patch_rows, feat_width = patches.shape
    tok_rows = patch_rows // 4
    score_scale = HEAD ** (-0.5)
    values = patches.astype(jnp.float32)
    row_mean = jnp.mean(values, -1, keepdims=True)
    ln_scale = lax.rsqrt(
        jnp.mean(values * values, -1, keepdims=True) - row_mean * row_mean + EPSILON
    )
    normed = (values - row_mean) * ln_scale
    merge_in = normed.astype(jnp.bfloat16).reshape(tok_rows, 4 * feat_width)
    first_tile = lax.all_gather(w_merge1, "seq", axis=1, tiled=True)
    first_flat = first_tile.reshape(4 * feat_width, first_tile.shape[2])
    hidden_pre = jnp.dot(merge_in, first_flat, preferred_element_type=jnp.float32)
    hidden = jax.nn.gelu(hidden_pre, approximate=False).astype(jnp.bfloat16)
    second_tile = lax.all_gather(w_merge2, "seq", axis=1, tiled=True)
    model_width = second_tile.shape[1]
    partial_value = jnp.dot(hidden, second_tile, preferred_element_type=jnp.float32)
    merged = lax.psum(partial_value.astype(jnp.bfloat16), "mp")
    merged_f = merged.astype(jnp.float32)
    rms_scale = lax.rsqrt(jnp.mean(merged_f * merged_f, -1, keepdims=True) + EPSILON)
    normed_tok = merged_f * rms_scale
    query_tile, keyval_tile = (
        lax.all_gather(w_query, "seq", axis=0, tiled=True),
        lax.all_gather(w_keyval, "seq", axis=0, tiled=True),
    )
    kv_part = keyval_tile.shape[2]
    keyval_flat = keyval_tile.reshape(model_width, 2 * kv_part)
    normed_bf = normed_tok.astype(jnp.bfloat16)
    queries = jnp.dot(normed_bf, query_tile, preferred_element_type=jnp.float32).astype(
        jnp.bfloat16
    )
    own_keyval = jnp.dot(normed_bf, keyval_flat, preferred_element_type=jnp.float32).astype(
        jnp.bfloat16
    )
    query_part = queries.shape[1]
    kv_local = kv_part // HEAD
    per_kv = query_part // HEAD // kv_local
    run_ids = sample_ids[0]
    run_len = run_ids.shape[0]
    own_start = lax.axis_index("seq") * tok_rows
    reach = min(lax.axis_size("seq") - 1, (run_len // 2 + 2 * tok_rows - 2) // tok_rows)
    pieces = [own_keyval]
    for offset in range(1, reach + 1):
        pieces.insert(0, fetch_earlier(own_keyval, offset))
    window_kv = jnp.concatenate(pieces, 0)
    window_rows = window_kv.shape[0]
    key_pos = own_start - reach * tok_rows + jnp.arange(window_rows, dtype=jnp.int32)
    padded_ids = jnp.concatenate([jnp.full((reach * tok_rows,), -1, jnp.int32), run_ids], 0)
    key_ids = lax.dynamic_slice_in_dim(padded_ids, own_start, window_rows, 0)
    total_rows = window_kv.shape[0]
    key_heads = window_kv[:, :kv_part].reshape(total_rows, kv_local, HEAD)
    value_heads = window_kv[:, kv_part:].reshape(total_rows, kv_local, HEAD)
    query_pos = own_start + jnp.arange(tok_rows, dtype=jnp.int32)
    own_ids = lax.dynamic_slice_in_dim(run_ids, own_start, tok_rows, 0)
    allowed = (query_pos[:, None] >= key_pos[None, :]) & (own_ids[:, None] == key_ids[None, :])
    query_heads = queries.reshape(tok_rows, kv_local, per_kv, HEAD)
    scores = (
        jnp.einsum("tkgd,ukd->kgtu", query_heads, key_heads, preferred_element_type=jnp.float32)
        * score_scale
    )
    scores = jnp.where(allowed, scores, -NEGATIVE)
    row_max = jnp.max(scores, -1, keepdims=True)
    shifted = jnp.exp(scores - row_max)
    soft = shifted / jnp.sum(shifted, -1, keepdims=True)
    soft_bf = soft.astype(jnp.bfloat16)
    attended = jnp.einsum(
        "kgtu,ukd->tkgd", soft_bf, value_heads, preferred_element_type=jnp.float32
    )
    grad_heads = attn_grad.reshape(tok_rows, kv_local, per_kv, HEAD)
    row_delta = jnp.sum(grad_heads.astype(jnp.float32) * attended, -1)
    dprob = jnp.einsum(
        "tkgd,ukd->kgtu", grad_heads, value_heads, preferred_element_type=jnp.float32
    )
    dscore = (soft * (dprob - jnp.transpose(row_delta, (1, 2, 0))[..., None])).astype(jnp.bfloat16)
    dquery = (
        jnp.einsum("kgtu,ukd->tkgd", dscore, key_heads, preferred_element_type=jnp.float32)
        * score_scale
    )
    dquery = dquery.astype(jnp.bfloat16).reshape(tok_rows, query_part)
    dkey_terms = (
        jnp.einsum("kgtu,tkgd->ukd", dscore, query_heads, preferred_element_type=jnp.float32)
        * score_scale
    )
    dvalue_terms = jnp.einsum(
        "kgtu,tkgd->ukd", soft_bf, grad_heads, preferred_element_type=jnp.float32
    )
    dkey = dkey_terms[reach * tok_rows :]
    dvalue = dvalue_terms[reach * tok_rows :]
    for offset in range(1, reach + 1):
        begin_row = (reach - offset) * tok_rows
        key_back, value_back = return_terms(
            (
                dkey_terms[begin_row : begin_row + tok_rows],
                dvalue_terms[begin_row : begin_row + tok_rows],
            ),
            offset,
        )
        dkey = dkey + key_back
        dvalue = dvalue + value_back
    grads_kv = jnp.concatenate(
        [
            dkey.astype(jnp.bfloat16).reshape(tok_rows, kv_part),
            dvalue.astype(jnp.bfloat16).reshape(tok_rows, kv_part),
        ],
        1,
    )
    dnormed_part = jnp.einsum("tc,dc->td", dquery, query_tile, preferred_element_type=jnp.float32)
    dnormed_part = dnormed_part + jnp.einsum(
        "tc,dc->td", grads_kv, keyval_flat, preferred_element_type=jnp.float32
    )
    dnormed = lax.psum(dnormed_part.astype(jnp.bfloat16), "mp").astype(jnp.float32)
    inner_mean = jnp.mean(dnormed * normed_tok, -1, keepdims=True)
    dmerged = (rms_scale * (dnormed - normed_tok * inner_mean)).astype(jnp.bfloat16)
    dhidden = jnp.einsum("td,hd->th", dmerged, second_tile, preferred_element_type=jnp.float32)
    dhidden_pre = (dhidden * gelu_grad(hidden_pre)).astype(jnp.bfloat16)
    dmerge_part = jnp.einsum(
        "th,fh->tf", dhidden_pre, first_flat, preferred_element_type=jnp.float32
    )
    dmerge_in = lax.psum_scatter(
        dmerge_part.reshape(patch_rows, feat_width).astype(jnp.bfloat16),
        "mp",
        scatter_dimension=0,
        tiled=True,
    ).astype(jnp.float32)
    share_rows = dmerge_in.shape[0]
    begin = lax.axis_index("mp") * share_rows
    own_normed = lax.dynamic_slice_in_dim(normed, begin, share_rows, 0)
    own_scale = lax.dynamic_slice_in_dim(ln_scale, begin, share_rows, 0)
    first_mean = jnp.mean(dmerge_in, -1, keepdims=True)
    second_mean = jnp.mean(dmerge_in * own_normed, -1, keepdims=True)
    patch_grad = own_scale * (dmerge_in - first_mean - own_normed * second_mean)
    return patch_grad.astype(jnp.bfloat16)


def solution(mesh):
    in_specs = (
        P(("group", "seq"), None),
        P(None, "seq", "mp"),
        P("mp", "seq"),
        P("seq", "mp"),
        P("seq", None, "mp"),
        P(("group", "seq"), "mp"),
        P("group", None),
    )
    out_specs = P(("group", "seq", "mp"), None)
    return jax.shard_map(local, mesh=mesh, in_specs=in_specs, out_specs=out_specs, check_vma=False)
```

profile of v0, /device:TPU:0, one launch (start us, length us, event | category | flops | bytes accessed | tf_op | source)
XLA Modules:
  0.0 488.3 jit_solution(8009914416394618098)
XLA Ops:
  9.1 1.4 fusion.20
  10.8 48.7 %all-gather.5.cloned.1.call-done = bf16[4,640,1280]{2,1,0:T(8,128)(2,1)} async-done(((bf16[4,160,1280]{2,1,0:T(8,128)(2,1)}), bf16[4,640,1280]{2,1,0:T(8,128)(2,1)}) %all-gather.5.cloned.1.call-update) | async-done | bytes 6553616 | tf_op jit(solution)/shard_map/all_gather | solution.py:47
  59.5 3.9 fusion.140
  63.4 67.9 %all-gather.7.cloned.1.call-done = bf16[1280,4096]{1,0:T(8,128)(2,1)} async-done(((bf16[1280,1024]{1,0:T(8,128)(2,1)}), bf16[1280,4096]{1,0:T(8,128)(2,1)}) %all-gather.7.cloned.1.call-update) | async-done | bytes 10485776 | tf_op jit(solution)/shard_map/all_gather | solution.py:51
  131.3 7.8 %convolution_convert_fusion = bf16[128,4096]{1,0:T(8,128)(2,1)} fusion(bf16[1280,4096]{1,0:T(8,128)(2,1)} %all-gather.7.cloned.1.call-done, f32[128,1280]{1,0:T(8,128)S(1)} %fusion.140), kind=kOutput, calls=%fused_computation.3 | convolution fusion | flops 1353351168 | bytes 12189696 | tf_op jit(solution)/shard_map/dot_general | solution.py:53
  139.9 51.3 %all-gather.9.cloned.1.call-done = bf16[4096,2,512]{2,1,0:T(2,128)(2,1)} async-done(((bf16[1024,2,512]{2,1,0:T(2,128)(2,1)}), bf16[4096,2,512]{2,1,0:T(2,128)(2,1)}) %all-gather.9.cloned.1.call-update) | async-done | bytes 8388624 | tf_op jit(solution)/shard_map/all_gather | solution.py:60
  191.1 9.3 %copy.52 = bf16[512,8,2,512]{3,1,2,0:T(8,128)(2,1)} copy(bf16[512,8,2,512]{3,2,1,0:T(2,128)(2,1)} %bitcast.81) | data formatting | bytes 16777216
  200.5 33.0 %all-reduce.4.cloned.1.call-done = bf16[128,4096]{1,0:T(8,128)(2,1)} async-done(((bf16[128,4096]{1,0:T(8,128)(2,1)}), bf16[128,4096]{1,0:T(8,128)(2,1)}) %all-reduce.4.cloned.1.call-update) | async-done | bytes 1048592 | tf_op jit(solution)/shard_map/psum | solution.py:54
  233.5 1.5 fusion.8
  235.0 5.1 %convolution_convert_fusion.3 = bf16[128,1024]{1,0:T(8,128)(2,1)S(1)} fusion(bf16[4096,1024]{1,0:T(8,128)(2,1)} %bitcast.79, bf16[128,4096]{1,0:T(8,128)(2,1)} %all-reduce.4.cloned.1.call-done, f32[128]{0:T(128)S(1)} %add_rsqrt_fusion.1), kind=kOutput, calls=%fused_computation.43 | convolution fusion | flops 1075445760 | bytes 9699840 | tf_op jit(solution)/shard_map/dot_general | solution.py:68
  240.1 1.6 collective-permute-start.2
  241.7 3.7 collective-permute-start.1
  245.4 1.5 collective-permute-start
  247.4 10.1 %collective-permute-done.1 = bf16[128,1024]{1,0:T(8,128)(2,1)S(1)} collective-permute-done((bf16[128,1024]{1,0:T(8,128)(2,1)S(1)}, bf16[128,1024]{1,0:T(8,128)(2,1)S(1)}, u32[]{:S(2)}, u32[]{:S(2)}) %collective-permute-start.1) | collective-permute-done | bytes 262176 | tf_op jit(solution)/shard_map/ppermute | solution.py:16
  257.5 8.7 %collective-permute-done = bf16[128,1024]{1,0:T(8,128)(2,1)S(1)} collective-permute-done((bf16[128,1024]{1,0:T(8,128)(2,1)S(1)}, bf16[128,1024]{1,0:T(8,128)(2,1)S(1)}, u32[]{:S(2)}, u32[]{:S(2)}) %collective-permute-start) | collective-permute-done | bytes 262176 | tf_op jit(solution)/shard_map/ppermute | solution.py:16
  267.3 77.9 %all-gather.11.cloned.1.call-done = bf16[4096,2048]{1,0:T(8,128)(2,1)} async-done(((bf16[1024,2048]{1,0:T(8,128)(2,1)}), bf16[4096,2048]{1,0:T(8,128)(2,1)}) %all-gather.11.cloned.1.call-update) | async-done | bytes 16777232 | tf_op jit(solution)/shard_map/all_gather | solution.py:59
  345.2 8.2 %convolution_convert_fusion.2 = bf16[128,2048]{1,0:T(8,128)(2,1)S(1)} fusion(bf16[4096,2048]{1,0:T(8,128)(2,1)} %all-gather.11.cloned.1.call-done, bf16[128,4096]{1,0:T(8,128)(2,1)S(1)} %copy-done, f32[128]{0:T(128)S(1)} %add_rsqrt_fusion.1), kind=kOutput, calls=%fused_computation.19 | convolution fusion | flops 2149318656 | bytes 18350592 | tf_op jit(solution)/shard_map/dot_general | solution.py:65
  354.4 4.5 fusion.137
  358.9 2.7 fusion.15
  361.6 1.8 fusion.139
  365.0 1.3 fusion.21
  366.3 1.8 fusion.138
  374.2 1.5 collective-permute-start.8
  375.7 11.7 %fusion.141 = f32[128,4096]{1,0:T(8,128)S(1)} fusion(bf16[128,2048]{0,1:T(8,128)(2,1)} %bitcast.87, bf16[4096,2048]{1,0:T(8,128)(2,1)} %all-gather.11.cloned.1.call-done), kind=kOutput, calls=%fused_computation.182 | convolution fusion | flops 2147483648 | bytes 19398656 | tf_op jit(solution)/shard_map/tc,dc->td/dot_general | solution.py:143
  387.4 1.3 collective-permute-start.7
  390.0 7.9 %collective-permute-done.7 = bf16[128,4,128]{0,2,1:T(8,128)(2,1)S(1)} collective-permute-done((bf16[128,4,128]{0,2,1:T(8,128)(2,1)S(1)}, bf16[128,4,128]{0,2,1:T(8,128)(2,1)S(1)}, u32[]{:S(2)}, u32[]{:S(2)}) %collective-permute-start.7) | collective-permute-done | bytes 131104 | tf_op jit(solution)/shard_map/ppermute | solution.py:16
  399.0 7.3 %fusion.1 = bf16[128,4096]{1,0:T(8,128)(2,1)} fusion(f32[128,4096]{1,0:T(8,128)S(1)} %fusion.141, bf16[4096,1024]{1,0:T(8,128)(2,1)} %bitcast.80, bf16[128,512]{0,1:T(8,128)(2,1)S(1)} %bitcast.93, bf16[128,512]{0,1:T(8,128)(2,1)S(1)} %bitcast.92), kind=kOutput, calls=%fused_computation.2 | convolution fusion | flops 1075314688 | bytes 11796480 | tf_op jit(solution)/shard_map/tc,dc->td/dot_general | solution.py:144
  406.3 40.4 %all-reduce.6.cloned.1.call-done = bf16[128,4096]{1,0:T(8,128)(2,1)} async-done(((bf16[128,4096]{1,0:T(8,128)(2,1)}), bf16[128,4096]{1,0:T(8,128)(2,1)}) %all-reduce.6.cloned.1.call-update) | async-done | bytes 1048592 | tf_op jit(solution)/shard_map/psum | solution.py:147
  446.8 1.8 fusion.9
  448.6 12.3 %convolution_convert_fusion.1 = bf16[128,2560]{1,0:T(8,128)(2,1)S(1)} fusion(bf16[2560,1280]{1,0:T(8,128)(2,1)} %bitcast.83, bf16[1280,4096]{1,0:T(8,128)(2,1)} %all-gather.7.cloned.1.call-done, bf16[128,4096]{1,0:T(8,128)(2,1)S(1)} %copy-done, bf16[128,4096]{1,0:T(8,128)(2,1)S(1)} %copy-done.5, f32[128]{0:T(128)S(1)} %broadcast_multiply_fusion.3, ...), kind=kOutput, calls=%fused_computation.9 | convolution fusion | flops 2186674176 | bytes 20448256 | tf_op jit(solution)/shard_map/th,fh->tf/dot_general | solution.py:152
  462.2 16.2 %reduce-scatter.2.cloned.1.call-done = bf16[256,640]{1,0:T(8,128)(2,1)} async-done(((bf16[512,640]{1,0:T(8,128)(2,1)}), bf16[256,640]{1,0:T(8,128)(2,1)}) %reduce-scatter.2.cloned.1.call-update) | async-done | bytes 327696 | tf_op jit(solution)/shard_map/reduce_scatter | solution.py:155
  479.5 1.9 fusion.35
  (72 shorter events, 18.7 us)
Async XLA Ops:
  6.5 53.0 %all-gather.5.cloned.1.call-start = ((), (), s32[]{:S(2)}) async-start(), calls=%async_computation.1 | async-start | bytes 8192000 | tf_op jit(solution)/shard_map/all_gather | solution.py:47
  7.3 1.5 copy-start.3
  7.3 124.0 %all-gather.7.cloned.1.call-start = ((), (), s32[]{:S(2)}) async-start(), calls=%async_computation.2 | async-start | bytes 13107200 | tf_op jit(solution)/shard_map/all_gather | solution.py:51
  8.0 183.1 %all-gather.9.cloned.1.call-start = ((), (), s32[]{:S(2)}) async-start(), calls=%async_computation.4 | async-start | bytes 10485760 | tf_op jit(solution)/shard_map/all_gather | solution.py:60
  8.8 224.7 %all-reduce.4.cloned.1.call-start = ((), (), s32[]{:S(2)}) async-start(), calls=%async_computation.3 | async-start | bytes 2097152 | tf_op jit(solution)/shard_map/psum | solution.py:54
  63.4 75.7 %copy-start.6 = (f32[128,1280]{1,0:T(8,128)}, f32[128,1280]{1,0:T(8,128)S(1)}, u32[]{:S(2)}) copy-start(f32[128,1280]{1,0:T(8,128)S(1)} %fusion.140) | copy-start | bytes 1966084
  139.1 0.7 copy-start.9
  139.1 206.1 %all-gather.11.cloned.1.call-start = ((), (), s32[]{:S(2)}) async-start(), calls=%async_computation.5 | async-start | bytes 20971520 | tf_op jit(solution)/shard_map/all_gather | solution.py:59
  139.7 307.1 %all-reduce.6.cloned.1.call-start = ((), (), s32[]{:S(2)}) async-start(), calls=%async_computation.6 | async-start | bytes 2097152 | tf_op jit(solution)/shard_map/psum | solution.py:147
  235.0 11.9 %copy-start.8 = (bf16[128,2048]{1,0:T(8,128)(2,1)S(1)}, bf16[128,2048]{1,0:T(8,128)(2,1)}, u32[]{:S(2)}) copy-start(bf16[128,2048]{1,0:T(8,128)(2,1)} %param.12) | copy-start | bytes 1572868
  240.1 7.3 %collective-permute-start.2 = (bf16[128,1024]{1,0:T(8,128)(2,1)S(1)}, bf16[128,1024]{1,0:T(8,128)(2,1)S(1)}, u32[]{:S(2)}, u32[]{:S(2)}) collective-permute-start(bf16[128,1024]{1,0:T(8,128)(2,1)S(1)} %convolution_convert_fusion.3), channel_id=1, source_target_pairs={{0,2},{2,4},{4,6},{1,3},{3,5},{5,7},{8,10},{10,12},{12,14},{9,11},... | collective-permute-start | bytes 786440 | tf_op jit(solution)/shard_map/ppermute | solution.py:16
  241.7 15.8 %collective-permute-start.1 = (bf16[128,1024]{1,0:T(8,128)(2,1)S(1)}, bf16[128,1024]{1,0:T(8,128)(2,1)S(1)}, u32[]{:S(2)}, u32[]{:S(2)}) collective-permute-start(bf16[128,1024]{1,0:T(8,128)(2,1)S(1)} %convolution_convert_fusion.3), channel_id=1, source_target_pairs={{0,4},{2,6},{1,5},{3,7},{8,12},{10,14},{9,13},{11,15},{16,20},{18,... | collective-permute-start | bytes 786440 | tf_op jit(solution)/shard_map/ppermute | solution.py:16
  245.4 20.8 %collective-permute-start = (bf16[128,1024]{1,0:T(8,128)(2,1)S(1)}, bf16[128,1024]{1,0:T(8,128)(2,1)S(1)}, u32[]{:S(2)}, u32[]{:S(2)}) collective-permute-start(bf16[128,1024]{1,0:T(8,128)(2,1)S(1)} %convolution_convert_fusion.3), channel_id=1, source_target_pairs={{0,6},{1,7},{8,14},{9,15},{16,22},{17,23},{24,30},{25,31}} | collective-permute-start | bytes 786440 | tf_op jit(solution)/shard_map/ppermute | solution.py:16
  266.4 78.8 %copy-start = (bf16[128,4096]{1,0:T(8,128)(2,1)S(1)}, bf16[128,4096]{1,0:T(8,128)(2,1)}, u32[]{:S(2)}) copy-start(bf16[128,4096]{1,0:T(8,128)(2,1)} %all-reduce.4.cloned.1.call-done) | copy-start | bytes 3145732
  361.6 2.6 copy-start.2
  365.0 1.3 copy-start.4
  369.0 18.4 %collective-permute-start.3 = (bf16[128,4,128]{0,2,1:T(8,128)(2,1)}, bf16[128,4,128]{0,2,1:T(8,128)(2,1)}, u32[]{:S(2)}, u32[]{:S(2)}) collective-permute-start(bf16[128,4,128]{0,2,1:T(8,128)(2,1)} %get-tuple-element.13), channel_id=1, source_target_pairs={{2,0},{4,2},{6,4},{3,1},{5,3},{7,5},{10,8},{12,10},{14,12},{11,9},... | collective-permute-start | bytes 393224 | tf_op jit(solution)/shard_map/ppermute | solution.py:16
  370.3 18.4 %collective-permute-start.5 = (bf16[128,4,128]{0,2,1:T(8,128)(2,1)}, bf16[128,4,128]{0,2,1:T(8,128)(2,1)}, u32[]{:S(2)}, u32[]{:S(2)}) collective-permute-start(bf16[128,4,128]{0,2,1:T(8,128)(2,1)} %get-tuple-element.14), channel_id=1, source_target_pairs={{6,0},{7,1},{14,8},{15,9},{22,16},{23,17},{30,24},{31,25}} | collective-permute-start | bytes 393224 | tf_op jit(solution)/shard_map/ppermute | solution.py:16
  371.6 17.1 %collective-permute-start.4 = (bf16[128,4,128]{0,2,1:T(8,128)(2,1)}, bf16[128,4,128]{0,2,1:T(8,128)(2,1)}, u32[]{:S(2)}, u32[]{:S(2)}) collective-permute-start(bf16[128,4,128]{0,2,1:T(8,128)(2,1)} %get-tuple-element.15), channel_id=1, source_target_pairs={{4,0},{6,2},{5,1},{7,3},{12,8},{14,10},{13,9},{15,11},{20,16},{22,... | collective-permute-start | bytes 393224 | tf_op jit(solution)/shard_map/ppermute | solution.py:16
  372.9 17.0 %collective-permute-start.6 = (bf16[128,4,128]{0,2,1:T(8,128)(2,1)S(1)}, bf16[128,4,128]{0,2,1:T(8,128)(2,1)}, u32[]{:S(2)}, u32[]{:S(2)}) collective-permute-start(bf16[128,4,128]{0,2,1:T(8,128)(2,1)S(1)} %get-tuple-element.16), channel_id=1, source_target_pairs={{2,0},{4,2},{6,4},{3,1},{5,3},{7,5},{10,8},{12,10},{14,12},{11,9},... | collective-permute-start | bytes 393224 | tf_op jit(solution)/shard_map/ppermute | solution.py:16
  374.2 15.7 %collective-permute-start.8 = (bf16[128,4,128]{0,2,1:T(8,128)(2,1)S(1)}, bf16[128,4,128]{0,2,1:T(8,128)(2,1)}, u32[]{:S(2)}, u32[]{:S(2)}) collective-permute-start(bf16[128,4,128]{0,2,1:T(8,128)(2,1)S(1)} %get-tuple-element.17), channel_id=1, source_target_pairs={{6,0},{7,1},{14,8},{15,9},{22,16},{23,17},{30,24},{31,25}} | collective-permute-start | bytes 393224 | tf_op jit(solution)/shard_map/ppermute | solution.py:16
  387.4 10.4 %collective-permute-start.7 = (bf16[128,4,128]{0,2,1:T(8,128)(2,1)S(1)}, bf16[128,4,128]{0,2,1:T(8,128)(2,1)S(1)}, u32[]{:S(2)}, u32[]{:S(2)}) collective-permute-start(bf16[128,4,128]{0,2,1:T(8,128)(2,1)S(1)} %get-tuple-element.18), channel_id=1, source_target_pairs={{4,0},{6,2},{5,1},{7,3},{12,8},{14,10},{13,9},{15,11},{20,16},{22,... | collective-permute-start | bytes 393224 | tf_op jit(solution)/shard_map/ppermute | solution.py:16
  406.2 42.3 %copy-start.7 = (f32[128,1280]{1,0:T(8,128)S(1)}, f32[128,1280]{1,0:T(8,128)}, u32[]{:S(2)}) copy-start(f32[128,1280]{1,0:T(8,128)} %copy-done.6) | copy-start | bytes 1966084
  406.3 72.1 %reduce-scatter.2.cloned.1.call-start = ((), (), s32[]{:S(2)}) async-start(), calls=%async_computation.7 | async-start | bytes 983040 | tf_op jit(solution)/shard_map/reduce_scatter | solution.py:155
  446.8 1.8 copy-start.5
  460.9 17.5 %copy-start.1 = (f32[512,640]{1,0:T(8,128)S(1)}, f32[512,640]{1,0:T(8,128)}, u32[]{:S(2)}) copy-start(f32[512,640]{1,0:T(8,128)} %get-tuple-element.11) | copy-start | bytes 3932164
Sparse Core Ops, SparseCore 0:
  8.9 50.5 all-gather.4
  61.1 70.1 all-gather.6
  132.8 58.2 all-gather.8
  193.3 40.1 all-reduce.3
  234.9 110.2 all-gather.10
  406.4 40.3 all-reduce.5
  462.3 16.0 reduce-scatter.1
where the time goes:
time: 489 us; the launch traced here: 488 us
  waiting for transfers between devices  365 us (75%)
  matrix products  66.9 us (14%)
  starting transfers between devices  15 us (3%)
  local copies, waits for them, and re-layouts  14.4 us (3%)
  between operations  13.9 us (3%)
  other arithmetic  13.4 us (3%)
    all_gather x1, waiting for transfers between devices, local(): lax.all_gather(w_query, 'seq', axis=0, tiled=True)  77.9 us
    all_gather x1, waiting for transfers between devices, local(): second_tile = lax.all_gather(w_merge2, 'seq', axis=1, tiled=True)  67.9 us
    all_gather x1, waiting for transfers between devices, local(): lax.all_gather(w_keyval, 'seq', axis=0, tiled=True)  51.3 us
    all_gather x1, waiting for transfers between devices, local(): first_tile = lax.all_gather(w_merge1, 'seq', axis=1, tiled=True)  48.7 us
    psum x1, waiting for transfers between devices, local(): lax.psum(dnormed_part.astype(jnp.bfloat16), 'mp').astype(jnp.float32)  40.4 us
    psum x1, waiting for transfers between devices, local(): merged = lax.psum(partial_value.astype(jnp.bfloat16), 'mp')  33 us
    ppermute x9, waiting for transfers between devices, shifted_2(): lax.ppermute(value, axis, [(source, source + steps) for source in range(i...  26.7 us
    reduce_scatter x1, waiting for transfers between devices, local(): lax.psum_scatter(dmerge_part.reshape(patch_rows, feat_width).astype(jnp.b...  16.2 us
  transfers between devices with their start and end apart: 16, of which 10 were waited for; matrix products, arithmetic and copies ran while one was open for 9% of the time, Pallas kernels for 0%

commit v1 on v0

--- a/solution.py
+++ b/solution.py
@@ -1,6 +1,8 @@
 import jax
 import jax.numpy as jnp
 from jax import lax
+from jax.experimental import pallas as pl
+from jax.experimental.pallas import tpu as pltpu
 from jax.sharding import PartitionSpec as P
 
 HEAD = 128
@@ -33,7 +35,7 @@
     )
 
 
-def local(patches, w_merge1, w_merge2, w_query, w_keyval, attn_grad, sample_ids):
+def local_gathered(patches, w_merge1, w_merge2, w_query, w_keyval, attn_grad, sample_ids):
     patch_rows, feat_width = patches.shape
     tok_rows = patch_rows // 4
     score_scale = HEAD ** (-0.5)
@@ -168,6 +170,549 @@
     return patch_grad.astype(jnp.bfloat16)
 
 
+BF16 = jnp.bfloat16
+F32 = jnp.float32
+LANES = 128
+
+
+def near(value):
+    count = lax.axis_size("seq")
+    return lax.ppermute(value, "seq", [(s, s ^ 1) for s in range(count)])
+
+
+def far(value):
+    count = lax.axis_size("seq")
+    return lax.ppermute(value, "seq", [(s, (s + count // 2) % count) for s in range(count)])
+
+
+def cross(value):
+    return lax.ppermute(value, "mp", [(0, 1), (1, 0)])
+
+
+def dot(a, b):
+    return jnp.dot(a, b, preferred_element_type=F32)
+
+
+def dot_t(a, b):
+    return lax.dot_general(a, b, (((1,), (1,)), ((), ())), preferred_element_type=F32)
+
+
+def dot_l(a, b):
+    return lax.dot_general(a, b, (((0,), (0,)), ((), ())), preferred_element_type=F32)
+
+
+def struct(shape, dtype):
+    return jax.ShapeDtypeStruct(shape, dtype)
+
+
+def whole(shape):
+    return pl.BlockSpec(shape, lambda *_: (0,) * len(shape))
+
+
+def call(body, name, grid, ins, outs, scratch, meta, *operands):
+    return pl.pallas_call(
+        body,
+        grid_spec=pltpu.PrefetchScalarGridSpec(
+            num_scalar_prefetch=1,
+            grid=grid,
+            in_specs=ins,
+            out_specs=[spec for spec, _ in outs],
+            scratch_shapes=scratch,
+        ),
+        out_shape=[shape for _, shape in outs],
+        compiler_params=pltpu.CompilerParams(
+            dimension_semantics=("arbitrary",) * len(grid), vmem_limit_bytes=48 << 20
+        ),
+        name=name,
+    )(meta, *operands)
+
+
+def full(shape, dtype):
+    return whole(shape), struct(shape, dtype)
+
+
+def layer_norm(values):
+    row_mean = jnp.mean(values, -1, keepdims=True)
+    scale = lax.rsqrt(jnp.mean(values * values, -1, keepdims=True) - row_mean * row_mean + EPSILON)
+    return (values - row_mean) * scale, scale
+
+
+def prepare(meta, patches, seqs):
+    rows, feats = patches.shape
+    toks, part = rows // 4, feats // seqs
+    tiles = feats // LANES
+
+    def body(meta, x, own, other, buf):
+        seq = meta[0] // 2
+        normed = layer_norm(x[...].astype(F32))[0]
+        for n in range(tiles):
+            buf[n] = normed[:, n * LANES : (n + 1) * LANES]
+        lanes = [
+            jnp.concatenate([buf[n, pl.ds(p, toks, stride=4), :] for n in range(tiles)], 1)
+            for p in range(4)
+        ]
+        for j in range(seqs):
+            cols = [v[:, j * part : (j + 1) * part] for v in lanes]
+            cols = jnp.concatenate(cols, 1).astype(BF16)
+            place = seq ^ j
+            for r in range(2):
+
+                @pl.when(place == r)
+                def _():
+                    own[r] = cols
+
+                @pl.when(place == r + 2)
+                def _():
+                    other[r] = cols
+
+    shape = (2, toks, 4 * part)
+    return call(
+        body, "prepare", (1,), [whole(patches.shape)], [full(shape, BF16)] * 2,
+        [pltpu.VMEM((tiles, rows, LANES), F32)], meta, patches,
+    )
+
+
+def first(meta, x, w, w_n, dtype):
+    _, toks, depth = x.shape
+    hid = w.shape[1]
+    bn = hid // 2
+
+    def body(_, x, w, w_n, out):
+        out[...] = (dot(x[0], w[...]) + dot(x[1], w_n[...])).astype(dtype)
+
+    col = pl.BlockSpec((depth, bn), lambda n, _: (0, n))
+    return call(
+        body, "first", (hid // bn,), [whole(x.shape), col, col],
+        [(pl.BlockSpec((toks, bn), lambda n, _: (0, n)), struct((toks, hid), dtype))], [],
+        meta, x, w, w_n,
+    )[0]
+
+
+def merge_hidden(meta, part, back, w, w_n):
+    toks, hid = part.shape
+    width = w.shape[1]
+    bn = width // 4
+
+    def body(_, part, back, w, w_n, pre, hidden, out):
+        @pl.when(pl.program_id(0) == 0)
+        def _():
+            total = part[...] + back[...].astype(F32)
+            pre[...] = total
+            hidden[...] = (total * 0.5 * (1.0 + lax.erf(total * 0.7071067811865476))).astype(BF16)
+
+        rows = hidden[...]
+        out[0] = dot(rows, w[...]).astype(BF16)
+        out[1] = dot(rows, w_n[...]).astype(BF16)
+
+    col = pl.BlockSpec((hid, bn), lambda n, _: (0, n))
+    return call(
+        body, "merge_hidden", (width // bn,), [whole(part.shape), whole(part.shape), col, col],
+        [full(part.shape, F32), full(part.shape, BF16),
+         (pl.BlockSpec((2, toks, bn), lambda n, _: (0, 0, n)), struct((2, toks, width), BF16))],
+        [], meta, part, back, w, w_n,
+    )
+
+
+def merge_far(meta, hidden, w, w_n):
+    toks, hid = hidden.shape
+    width = w.shape[1]
+    bn = width // 4
+
+    def body(_, hidden, w, w_n, out):
+        out[0] = dot(hidden[...], w[...]).astype(BF16)
+        out[1] = dot(hidden[...], w_n[...]).astype(BF16)
+
+    col = pl.BlockSpec((hid, bn), lambda n, _: (0, n))
+    return call(
+        body, "merge_far", (width // bn,), [whole(hidden.shape), col, col],
+        [(pl.BlockSpec((2, toks, bn), lambda n, _: (0, 0, n)), struct((2, toks, width), BF16))],
+        [], meta, hidden, w, w_n,
+    )[0]
+
+
+def column_specs(weights, swap):
+    wq, _, wkv, _ = weights
+    width = wq.shape[0]
+    q_own, kv_own = wq.shape[1] // 4, wkv.shape[1] // 8
+
+    def place(c, meta):
+        return ((meta[0] // 2) ^ (2 * swap)) ^ c
+
+    q = pl.BlockSpec((width, q_own), lambda c, meta: (0, place(c, meta)))
+    k = pl.BlockSpec((width, kv_own), lambda c, meta: (0, place(c, meta)))
+    v = pl.BlockSpec((width, kv_own), lambda c, meta: (0, 4 + place(c, meta)))
+    operands = [wq, weights[1], wkv, weights[3], wkv, weights[3]]
+    return [q, q, k, k, v, v], operands, q_own, kv_own
+
+
+def project_send(meta, mine, other, weights):
+    _, toks, width = mine.shape
+    specs, operands, q_own, kv_own = column_specs(weights, 1)
+    cols = q_own + 2 * kv_own
+
+    def body(_, mine, other, q, qn, k, kn, v, vn, merged, squares, out):
+        @pl.when(pl.program_id(0) == 0)
+        def _():
+            total = (mine[...].astype(F32) + other[...].astype(F32)).astype(BF16)
+            merged[...] = total
+            wide = total.astype(F32)
+            squares[...] = jnp.sum(jnp.sum(wide * wide, 0), -1, keepdims=True)
+
+        a, b = merged[0], merged[1]
+        out[0, :, :q_own] = (dot(a, q[...]) + dot(b, qn[...])).astype(BF16)
+        out[0, :, q_own : q_own + kv_own] = (dot(a, k[...]) + dot(b, kn[...])).astype(BF16)
+        out[0, :, q_own + kv_own :] = (dot(a, v[...]) + dot(b, vn[...])).astype(BF16)
+
+    return call(
+        body, "project_send", (2,), [whole(mine.shape)] * 2 + specs,
+        [full(mine.shape, BF16), full((toks, 1), F32),
+         (pl.BlockSpec((1, toks, cols), lambda c, _: (c, 0, 0)), struct((2, toks, cols), BF16))],
+        [], meta, mine, other, *operands,
+    )
+
+
+def project_keep(meta, merged, weights):
+    _, toks, width = merged.shape
+    specs, operands, q_own, kv_own = column_specs(weights, 0)
+    cols = q_own + 2 * kv_own
+
+    def body(_, merged, q, qn, k, kn, v, vn, out):
+        a, b = merged[0], merged[1]
+        out[0, :, :q_own] = dot(a, q[...]) + dot(b, qn[...])
+        out[0, :, q_own : q_own + kv_own] = dot(a, k[...]) + dot(b, kn[...])
+        out[0, :, q_own + kv_own :] = dot(a, v[...]) + dot(b, vn[...])
+
+    return call(
+        body, "project_keep", (2,), [whole(merged.shape)] + specs,
+        [(pl.BlockSpec((1, toks, cols), lambda c, _: (c, 0, 0)), struct((2, toks, cols), F32))],
+        [], meta, merged, *operands,
+    )[0]
+
+
+def scale_heads(meta, keeps, gots, rms):
+    _, toks, cols = gots[0].shape
+
+    def body(_, k0, k1, g0, g1, rms, mine, side):
+        for i, (k, g) in enumerate(((k0, g0), (k1, g1))):
+            total = (k[...] + g[...].astype(F32)) * rms[i][None]
+            mine[i] = total[0].astype(BF16)
+            side[i] = total[1].astype(BF16)
+
+    return call(
+        body, "scale_heads", (1,), [whole(gots[0].shape)] * 4 + [whole(rms.shape)],
+        [full((2, toks, cols), BF16)] * 2, [], meta, *keeps, *gots, rms,
+    )
+
+
+def attention(meta, mine, side, grad_mine, grad_side, ids_row, ids_col):
+    _, toks, cols = mine.shape
+    q_own = grad_mine.shape[2]
+    kv_own = (cols - q_own) // 2
+    heads, per_kv = kv_own // HEAD, q_own // kv_own
+    scale = HEAD ** (-0.5)
+    tiles = 4
+    lanes = per_kv * toks
+
+    def body(meta, mine, side, g_mine, g_side, ids_row, ids_col, d_own, d_far, d_side, dk_buf, dv_buf):
+        seq = meta[0] // 2
+        order = [seq, seq ^ 2, seq ^ 1, seq ^ 3]
+        qkv = [mine.at[0], mine.at[1], side.at[0], side.at[1]]
+        grads = [g_mine.at[0], g_mine.at[1], g_side.at[0], g_side.at[1]]
+        outs = [d_own, d_far, d_side.at[0], d_side.at[1]]
+        key_pos = jnp.concatenate(
+            [o * toks + lax.broadcasted_iota(jnp.int32, (toks, 1), 0) for o in order], 0
+        )
+        key_ids = jnp.concatenate([ids_col[o] for o in order], 0)
+        for h in range(heads):
+            ks = slice(q_own + h * HEAD, q_own + (h + 1) * HEAD)
+            vs = slice(q_own + kv_own + h * HEAD, q_own + kv_own + (h + 1) * HEAD)
+            keys = jnp.concatenate([r[:, ks] for r in qkv], 0)
+            vals = jnp.concatenate([r[:, vs] for r in qkv], 0)
+            for i in range(tiles):
+                qs = [slice((h * per_kv + g) * HEAD, (h * per_kv + g + 1) * HEAD) for g in range(per_kv)]
+                q = jnp.concatenate([qkv[i][:, s] for s in qs], 0)
+                g = jnp.concatenate([grads[i][:, s] for s in qs], 0)
+                pos = order[i] * toks + lax.broadcasted_iota(jnp.int32, (1, toks), 1)
+                allowed = (pos >= key_pos) & (ids_row[order[i]] == key_ids)
+                allowed = jnp.concatenate([allowed] * per_kv, 1)
+                s = jnp.where(allowed, dot_t(keys, q) * scale, -NEGATIVE)
+                e = jnp.exp(s - jnp.max(s, 0, keepdims=True))
+                soft = e / jnp.sum(e, 0, keepdims=True)
+                soft_bf = soft.astype(BF16)
+                dprob = dot_t(vals, g)
+                delta = jnp.sum(soft_bf.astype(F32) * dprob, 0, keepdims=True)
+                ds = (soft * (dprob - delta)).astype(BF16)
+                dk, dv = dot(ds, q), dot(soft_bf, g)
+                if i == 0:
+                    dk_buf[...], dv_buf[...] = dk, dv
+                else:
+                    dk_buf[...] += dk
+                    dv_buf[...] += dv
+                dq = (dot_l(ds, keys) * scale).astype(BF16)
+                for n, s_ in enumerate(qs):
+                    outs[i][:, s_] = dq[n * toks : (n + 1) * toks]
+            for i in range(tiles):
+                outs[i][:, ks] = (dk_buf[i * toks : (i + 1) * toks] * scale).astype(BF16)
+                outs[i][:, vs] = dv_buf[i * toks : (i + 1) * toks].astype(BF16)
+
+    shape = (toks, cols)
+    return call(
+        body, "attention", (1,),
+        [whole(a.shape) for a in (mine, side, grad_mine, grad_side, ids_row, ids_col)],
+        [full(shape, BF16), full(shape, BF16), full((2,) + shape, BF16)],
+        [pltpu.VMEM((tiles * toks, HEAD), F32)] * 2,
+        meta, mine, side, grad_mine, grad_side, ids_row, ids_col,
+    )
+
+
+def spread(a, q, k, v, q_own, kv_own):
+    return (
+        dot_t(a[:, :q_own], q[...])
+        + dot_t(a[:, q_own : q_own + kv_own], k[...])
+        + dot_t(a[:, q_own + kv_own :], v[...])
+    )
+
+
+def dnormed_mine(meta, d_own, d_far, d_side, weights):
+    toks, cols = d_own.shape
+    specs, operands, q_own, kv_own = column_specs(weights, 0)
+    width = weights[0].shape[0]
+
+    def body(_, own, other, side, q, qn, k, kn, v, vn, acc):
+        @pl.when(pl.program_id(0) == 0)
+        def _():
+            a = jnp.concatenate([own[...], other[...]], 0)
+            acc[:, :width] = spread(a, q, k, v, q_own, kv_own)
+            acc[:, width:] = spread(a, qn, kn, vn, q_own, kv_own)
+
+        @pl.when(pl.program_id(0) == 1)
+        def _():
+            a = side[...].reshape(2 * toks, cols)
+            acc[:, :width] += spread(a, q, k, v, q_own, kv_own)
+            acc[:, width:] += spread(a, qn, kn, vn, q_own, kv_own)
+
+    return call(
+        body, "dnormed_mine", (2,),
+        [whole(d_own.shape)] * 2 + [whole(d_side.shape)] + specs,
+        [full((2 * toks, 2 * width), F32)], [], meta, d_own, d_far, d_side, *operands,
+    )[0]
+
+
+def dnormed_rest(meta, acc, chunk, got, got_side, merged, rms, weights):
+    toks, cols = got.shape
+    specs, operands, q_own, kv_own = column_specs(weights, 1)
+    width = weights[0].shape[0]
+
+    def body(_, acc, got, got_side, merged, rms, q, qn, k, kn, v, vn, out, inner, buf):
+        @pl.when(pl.program_id(0) == 0)
+        def _():
+            a = got[...]
+            buf[0] = acc[:, :width] + spread(a, q, k, v, q_own, kv_own)
+            buf[1] = acc[:, width:] + spread(a, qn, kn, vn, q_own, kv_own)
+
+        @pl.when(pl.program_id(0) == 1)
+        def _():
+            a = got_side[...]
+            total = jnp.zeros((toks, 1), F32)
+            for i, (x, y, z) in enumerate(((q, k, v), (qn, kn, vn))):
+                part = (buf[i] + spread(a, x, y, z, q_own, kv_own)).astype(BF16)
+                out[i] = part
+                total += jnp.sum(part.astype(F32) * merged[i].astype(F32), -1, keepdims=True)
+            inner[...] = total * rms[...]
+
+    return call(
+        body, "dnormed_rest", (2,),
+        [pl.BlockSpec((toks, 2 * width), lambda c, _: (chunk, 0)), whole(got.shape),
+         whole(got.shape), whole(merged.shape), whole(rms.shape)] + specs,
+        [full((2, toks, width), BF16), full((toks, 1), F32)],
+        [pltpu.VMEM((2, toks, width), F32)],
+        meta, acc, got, got_side, merged, rms, *operands,
+    )
+
+
+def dhidden_of(meta, part, other, merged, rms, inner, w, w_n, tail=None):
+    _, toks, width = part.shape
+    hid = w.shape[0]
+    bn = hid // 5 if hid % 640 == 0 else hid
+
+    def body(_, part, other, merged, rms, inner, w, w_n, *rest):
+        out, buf = rest[-2:]
+
+        @pl.when(pl.program_id(0) == 0)
+        def _():
+            dnormed = part[...].astype(F32) + other[...].astype(F32)
+            normed = merged[...].astype(F32) * rms[...][None]
+            buf[...] = (rms[...][None] * (dnormed - normed * inner[...][None])).astype(BF16)
+
+        total = dot_t(buf[0], w[...]) + dot_t(buf[1], w_n[...])
+        if tail is not None:
+            back, pre = rest[:2]
+            total = (total + back[...].astype(F32)) * gelu_grad(pre[...])
+        out[...] = total.astype(BF16)
+
+    row = pl.BlockSpec((bn, width), lambda n, _: (n, 0))
+    col = pl.BlockSpec((toks, bn), lambda n, _: (0, n))
+    return call(
+        body, "dhidden", (hid // bn,),
+        [whole(part.shape)] * 3 + [whole(rms.shape)] * 2 + [row, row] + [col] * len(tail or ()),
+        [(col, struct((toks, hid), BF16))], [pltpu.VMEM(part.shape, BF16)],
+        meta, part, other, merged, rms, inner, w, w_n, *(tail or ()),
+    )[0]
+
+
+def dmerge(meta, d_own, d_far, w, w_n):
+    toks, hid = d_own.shape
+    depth = w.shape[0]
+    half = toks // 2
+    bn = depth // 5 if depth % 640 == 0 else depth
+
+    def body(meta, own, other, w, w_n, send, keep):
+        mp = meta[0] % 2
+        for out, start in ((send, (1 - mp) * half), (keep, mp * half)):
+            rows = pl.ds(pl.multiple_of(start, half), half)
+            a = jnp.concatenate([own[rows, :], other[rows, :]], 0)
+            out[0] = dot_t(a, w[...]).astype(out.dtype)
+            out[1] = dot_t(a, w_n[...]).astype(out.dtype)
+
+    row = pl.BlockSpec((bn, hid), lambda n, _: (n, 0))
+    col = pl.BlockSpec((2, toks, bn), lambda n, _: (0, 0, n))
+    return call(
+        body, "dmerge", (depth // bn,), [whole(d_own.shape)] * 2 + [row, row],
+        [(col, struct((2, toks, depth), BF16)), (col, struct((2, toks, depth), BF16))], [],
+        meta, d_own, d_far, w, w_n,
+    )
+
+
+def finish(meta, keep, got, other, patches, seqs):
+    rows, feats = patches.shape
+    share = rows // 2
+    toks = share // 4
+    part = feats // seqs
+    tiles = feats // LANES
+
+    def body(meta, keep, got, other, x, out, blocks, buf):
+        seq = meta[0] // 2
+        for r in range(2):
+            blocks[r] = keep[r, :toks].astype(F32) + got[r, :toks].astype(F32)
+            blocks[r + 2] = other[r].astype(F32)
+        cols = [blocks[seq ^ j] for j in range(seqs)]
+        for p in range(4):
+            row = jnp.concatenate([c[:, p * part : (p + 1) * part] for c in cols], 1)
+            for n in range(tiles):
+                buf[n, pl.ds(p, toks, stride=4), :] = row[:, n * LANES : (n + 1) * LANES]
+        grad = jnp.concatenate([buf[n] for n in range(tiles)], 1)
+        normed, scale = layer_norm(x[...].astype(F32))
+        first_mean = jnp.mean(grad, -1, keepdims=True)
+        second_mean = jnp.mean(grad * normed, -1, keepdims=True)
+        out[...] = (scale * (grad - first_mean - normed * second_mean)).astype(BF16)
+
+    return call(
+        body, "finish", (1,),
+        [whole(keep.shape), whole(got.shape), whole(other.shape),
+         pl.BlockSpec((share, feats), lambda _, meta: (meta[0] % 2, 0))],
+        [full((share, feats), BF16)],
+        [pltpu.VMEM((seqs, toks, 4 * part), F32), pltpu.VMEM((tiles, share, LANES), F32)],
+        meta, keep, got, other, patches,
+    )[0]
+
+
+def local_resident(patches, w_merge1, w_merge2, w_query, w_keyval, attn_grad, sample_ids):
+    patch_rows, feat_width = patches.shape
+    toks = patch_rows // 4
+    seqs = lax.axis_size("seq")
+    seq = lax.axis_index("seq")
+    meta = jnp.full((1,), seq * 2 + lax.axis_index("mp"), jnp.int32)
+    hid = w_merge1.shape[2]
+    width = w_merge2.shape[1]
+    model_width = width * seqs
+    q_own = w_query.shape[1] // seqs
+
+    w1 = w_merge1.reshape(-1, hid)
+    wkv = w_keyval.reshape(width, -1)
+    w1_n = near(w1)
+    x_own, x_out = prepare(meta, patches, seqs)
+    x_far = far(x_out)
+    w2 = w_merge2
+    w2_n = near(w2)
+    weights = (w_query, near(w_query), wkv, near(wkv))
+
+    part_own = first(meta, x_own, w1, w1_n, F32)
+    part_far = first(meta, x_far, w1, w1_n, BF16)
+    back = far(part_far)
+    hidden_pre, hidden, mine_own = merge_hidden(meta, part_own, back, w2, w2_n)
+    hidden_far = far(hidden)
+    other_own = cross(mine_own)
+    mine_far = merge_far(meta, hidden_far, w2, w2_n)
+    other_far = cross(mine_far)
+
+    mine_own, attn_grad = lax.optimization_barrier((mine_own, attn_grad))
+    ahead, core = seq // 2, seq % 2
+    grads = attn_grad.reshape(toks, 2, 2, q_own)
+
+    def pick(array, index, axis):
+        return lax.dynamic_index_in_dim(array, index, axis, keepdims=False)
+
+    grads = jnp.transpose(grads, (1, 2, 0, 3))
+    grads_keep = pick(grads, ahead, 0)
+    grads_got = far(pick(grads, 1 - ahead, 0))
+    grad_mine = jnp.stack([pick(grads_keep, core, 0), pick(grads_got, core, 0)], 0)
+    grad_side = near(jnp.stack([pick(grads_keep, 1 - core, 0), pick(grads_got, 1 - core, 0)], 0))
+
+    merged_own, sq_own, send_own = project_send(meta, mine_own, other_own, weights)
+    got_far = far(send_own)
+    keep_own = project_keep(meta, merged_own, weights)
+    merged_far, sq_far, send_far = project_send(meta, mine_far, other_far, weights)
+    got_own = far(send_far)
+    squares = jnp.stack([sq_own, sq_far], 0)
+    squares_got = far(squares)
+    keep_far = project_keep(meta, merged_far, weights)
+    rms = lax.rsqrt((squares + squares_got[::-1]) * (1.0 / model_width) + EPSILON)
+    qkv_mine, qkv_out = scale_heads(meta, (keep_own, keep_far), (got_own, got_far), rms)
+    qkv_side = near(qkv_out)
+
+    run_ids = sample_ids.reshape(seqs, toks)
+    d_own, d_far, d_out = attention(
+        meta, qkv_mine, qkv_side, grad_mine, grad_side, run_ids[:, None, :], run_ids[:, :, None]
+    )
+    d_far_got = far(d_own)
+    d_own_got = far(d_far)
+    d_side = near(d_out)
+    d_far_got_side = far(d_side[0])
+    d_own_got_side = far(d_side[1])
+    acc = dnormed_mine(meta, d_own, d_far, d_side, weights)
+    dn_far, in_far = dnormed_rest(
+        meta, acc, 1, d_far_got, d_far_got_side, merged_far, rms[1], weights
+    )
+    dn_far_got = cross(dn_far)
+    dn_own, in_own = dnormed_rest(
+        meta, acc, 0, d_own_got, d_own_got_side, merged_own, rms[0], weights
+    )
+    dn_own_got = cross(dn_own)
+    inner = jnp.stack([in_own, in_far], 0)
+    inner = inner + cross(inner)
+    inner = (inner + far(inner)[::-1]) * (1.0 / model_width)
+    dh_far = dhidden_of(meta, dn_far, dn_far_got, merged_far, rms[1], inner[1], w2, w2_n)
+    dh_back = far(dh_far)
+    dpre_own = dhidden_of(
+        meta, dn_own, dn_own_got, merged_own, rms[0], inner[0], w2, w2_n, (dh_back, hidden_pre)
+    )
+    dpre_far = far(dpre_own)
+    send, keep = dmerge(meta, dpre_own, dpre_far, w1, w1_n)
+    got = cross(send)
+    half = toks // 2
+    other = (keep[:, half:].astype(F32) + got[:, half:].astype(F32)).astype(BF16)
+    return finish(meta, keep, got, far(other), patches, seqs)
+
+
+def local(patches, w_merge1, w_merge2, w_query, w_keyval, attn_grad, sample_ids):
+    seqs = lax.axis_size("seq")
+    kv_heads = w_keyval.shape[2] // HEAD
+    plan = local_gathered
+    if seqs == 4 and lax.axis_size("mp") == 2 and kv_heads % seqs == 0:
+        plan = local_resident
+    return plan(patches, w_merge1, w_merge2, w_query, w_keyval, attn_grad, sample_ids)
+
+
 def solution(mesh):
     in_specs = (
         P(("group", "seq"), None),

time: 489 us -> 193 us (0.39)
  waiting for transfers between devices: 365 us -> 72.8 us
  matrix products: 66.9 us -> 0 us
  Pallas kernels: 0 us -> 66.3 us
  starting transfers between devices: 15 us -> 32.6 us
  between operations: 13.9 us -> 0.32 us
  other arithmetic: 13.4 us -> 3.42 us
    all_gather x4 -> x0, waiting for transfers between devices: 246 us -> none  [the longest x1 77.9 us: local(): lax.all_gather(w_query, 'seq', axis=0, tiled=True)]
    psum x2 -> x0, waiting for transfers between devices: 73.5 us -> none  [the longest x1 40.4 us: local(): lax.psum(dnormed_part.astype(jnp.bfloat16), 'mp').astype(jnp.float32)]
    pallas_call x0 -> x18, Pallas kernels: none -> 66.3 us  [call(): pl.pallas_call(body, grid_spec=pltpu.PrefetchScalarGridSpec(num_scalar_pr...]
    dot_general x12 -> x0, matrix products: 62.4 us -> none  [the longest x1 12.3 us: local(): jnp.einsum('th,fh->tf', dhidden_pre, first_flat, preferred_element_type=j...]
    ppermute x9 -> x28, waiting for transfers between devices: 26.7 us -> 72.8 us  [the longest x15 43.4 us: far(): lax.ppermute(value, 'seq', [(s, (s + count // 2) % count) for s in range(...]
    ppermute x9 -> x28, starting transfers between devices: 14.8 us -> 32.6 us  [the longest x15 23.5 us: far(): lax.ppermute(value, 'seq', [(s, (s + count // 2) % count) for s in range(...]
    reduce_scatter x1 -> x0, waiting for transfers between devices: 16.2 us -> none  [local(): lax.psum_scatter(dmerge_part.reshape(patch_rows, feat_width).astype(jnp.b...]
    convert_element_type x4 -> x1, other arithmetic: 6.9 us -> 0.04 us  [local_resident(): (keep[:, half:].astype(F32) + got[:, half:].astype(F32)).astype(BF16)]
  transfers between devices with their start and end apart: 16 -> 28, of which waited for: 10 -> 15; matrix products, arithmetic and copies ran while one was open for 9% -> 8% of each run, Pallas kernels for 0% -> 24%
where the time goes in v1:
time: 193 us; the launch traced here: 192 us
  waiting for transfers between devices  72.8 us (38%)
  Pallas kernels  66.3 us (34%)
  starting transfers between devices  32.6 us (17%)
  local copies, waits for them, and re-layouts  16.5 us (9%)
  other arithmetic  3.42 us (2%)
    pallas_call x18, Pallas kernels, call(): pl.pallas_call(body, grid_spec=pltpu.PrefetchScalarGridSpec(num_scalar_pr...  66.3 us
    ppermute x15, waiting for transfers between devices, far(): lax.ppermute(value, 'seq', [(s, (s + count // 2) % count) for s in range(...  43.4 us
    ppermute x6, waiting for transfers between devices, cross(): return lax.ppermute(value, 'mp', [(0, 1), (1, 0)])  29.4 us
    ppermute x15, starting transfers between devices, far(): lax.ppermute(value, 'seq', [(s, (s + count // 2) % count) for s in range(...  23.5 us
    unnamed x32, local copies, waits for them, and re-layouts  8.3 us
    ppermute x6, starting transfers between devices, cross(): return lax.ppermute(value, 'mp', [(0, 1), (1, 0)])  7.47 us
    another operation x4, local copies, waits for them, and re-layouts  4.14 us
  transfers between devices with their start and end apart: 28, of which 15 were waited for; matrix products, arithmetic and copies ran while one was open for 8% of the time, Pallas kernels for 24%

profile of v1, /device:TPU:0, one launch (start us, length us, event | category | flops | bytes accessed | tf_op | source)
XLA Modules:
  0.0 191.9 jit_solution(10476089262091273060)
XLA Ops:
  1.0 2.2 %copy.68 = bf16[128,8,2,512]{3,1,2,0:T(8,128)(2,1)S(1)} copy(bf16[128,8,2,512]{3,2,1,0:T(2,128)(2,1)} %bitcast.61) | data formatting | bytes 4194304
  4.3 3.1 %collective-permute-start.1 = (bf16[2,128,640]{2,1,0:T(8,128)(2,1)S(1)}, bf16[2,128,640]{2,1,0:T(8,128)(2,1)S(1)}, u32[]{:S(2)}, u32[]{:S(2)}) collective-permute-start(bf16[2,128,640]{2,1,0:T(8,128)(2,1)S(1)} %get-tuple-element.30), channel_id=1, source_target_pairs={{0,4},{2,6},{4,0},{6,2},{1,5},{3,7},{5,1},{7,3},{8,12},{10,14},{12... | collective-permute-start | bytes 983048 | tf_op jit(solution)/shard_map/ppermute | solution.py:185
  7.4 7.9 %collective-permute-done.1.x = bf16[2,128,640]{2,1,0:T(8,128)(2,1)S(1)} collective-permute-done((bf16[2,128,640]{2,1,0:T(8,128)(2,1)S(1)}, bf16[2,128,640]{2,1,0:T(8,128)(2,1)S(1)}, u32[]{:S(2)}, u32[]{:S(2)}) %collective-permute-start.1) | collective-permute-done | bytes 327712 | tf_op jit(solution)/shard_map/ppermute | solution.py:185
  16.7 2.3 %first.3 = bf16[128,1280]{1,0:T(8,128)(2,1)S(1)} custom-call(s32[1]{0:T(128)} %bitcast.meta._, bf16[2,128,640]{2,1,0:T(8,128)(2,1)S(1)} %collective-permute-done.1.x, bf16[640,1280]{1,0:T(8,128)(2,1)S(1)} %bitcast.44, bf16[640,1280]{1,0:T(8,128)(2,1)} %collective-permute-done.w_n), custom_call_target="tpu_custom_call" | custom-call | tf_op jit(solution)/shard_map/first/pallas_call | solution.py:213
  20.8 2.4 %first.2.part = f32[128,1280]{1,0:T(8,128)S(1)} custom-call(s32[1]{0:T(128)} %bitcast.meta._, bf16[2,128,640]{2,1,0:T(8,128)(2,1)S(1)} %get-tuple-element.29.x, bf16[640,1280]{1,0:T(8,128)(2,1)S(1)} %bitcast.45, bf16[640,1280]{1,0:T(8,128)(2,1)} %collective-permute-done.w_n), custom_call_target="tpu_custom_call" | custom-call | tf_op jit(solution)/shard_map/first/pallas_call | solution.py:213
  23.2 5.2 %collective-permute-done.2.back = bf16[128,1280]{1,0:T(8,128)(2,1)S(1)} collective-permute-done((bf16[128,1280]{1,0:T(8,128)(2,1)S(1)}, bf16[128,1280]{1,0:T(8,128)(2,1)S(1)}, u32[]{:S(2)}, u32[]{:S(2)}) %collective-permute-start.2) | collective-permute-done | bytes 327712 | tf_op jit(solution)/shard_map/ppermute | solution.py:185
  28.4 4.6 %merge_hidden.1 = (f32[128,1280]{1,0:T(8,128)S(1)}, bf16[128,1280]{1,0:T(8,128)(2,1)S(1)}, bf16[2,128,1024]{2,1,0:T(8,128)(2,1)}) custom-call(s32[1]{0:T(128)} %bitcast.meta._, f32[128,1280]{1,0:T(8,128)S(1)} %first.2.part, bf16[128,1280]{1,0:T(8,128)(2,1)S(1)} %collective-permute-done.2.back, bf16[1280,1024]{1,0:T(8,128)(2,1)S(1)} %copy-done, ...), custom_call_target="tpu_custom_call" | custom-call | tf_op jit(solution)/shard_map/merge_hidden/pallas_call | solution.py:213
  34.8 6.7 %collective-permute-done.7.hidden = bf16[128,1280]{1,0:T(8,128)(2,1)S(1)} collective-permute-done((bf16[128,1280]{1,0:T(8,128)(2,1)S(1)}, bf16[128,1280]{1,0:T(8,128)(2,1)S(1)}, u32[]{:S(2)}, u32[]{:S(2)}) %collective-permute-start.7) | collective-permute-done | bytes 327712 | tf_op jit(solution)/shard_map/ppermute | solution.py:185
  41.5 3.6 %merge_far.1.mine = bf16[2,128,1024]{2,1,0:T(8,128)(2,1)S(1)} custom-call(s32[1]{0:T(128)} %bitcast.meta._, bf16[128,1280]{1,0:T(8,128)(2,1)S(1)} %collective-permute-done.7.hidden, bf16[1280,1024]{1,0:T(8,128)(2,1)S(1)} %copy-done, bf16[1280,1024]{1,0:T(8,128)(2,1)} %collective-permute-done.3.w_n), custom_call_target="tpu_custom_call" | custom-call | tf_op jit(solution)/shard_map/merge_far/pallas_call | solution.py:213
  47.2 2.0 %copy.54 = bf16[128,2048]{0,1:T(8,128)(2,1)} copy(bf16[128,2048]{1,0:T(8,128)(2,1)} %param.12) | data formatting | bytes 1048576 | tf_op jit(solution)/shard_map/optimization_barrier | solution.py:648
  49.3 10.7 %collective-permute-done.8.other = bf16[2,128,1024]{2,1,0:T(8,128)(2,1)S(1)} collective-permute-done((bf16[2,128,1024]{2,1,0:T(8,128)(2,1)S(1)}, bf16[2,128,1024]{2,1,0:T(8,128)(2,1)S(1)}, u32[]{:S(2)}, u32[]{:S(2)}) %collective-permute-start.8) | collective-permute-done | bytes 524320 | tf_op jit(solution)/shard_map/ppermute | solution.py:189
  61.8 4.2 %project_send.3 = (bf16[2,128,1024]{2,1,0:T(8,128)(2,1)S(1)}, f32[128,1]{1,0:T(8,128)S(1)}, bf16[2,128,768]{2,1,0:T(8,128)(2,1)}) custom-call(s32[1]{0:T(128)} %bitcast.meta._, bf16[2,128,1024]{2,1,0:T(8,128)(2,1)S(1)} %merge_far.1.mine, bf16[2,128,1024]{2,1,0:T(8,128)(2,1)S(1)} %copy-done.10, bf16[1024,2048]{1,0:T(8,128)(2,1)} %q.13, ...), custom_call_target="tpu_custom_call" | custom-call | tf_op jit(solution)/shard_map/project_send/pallas_call | solution.py:213
  68.3 4.6 %project_send.2 = (bf16[2,128,1024]{2,1,0:T(8,128)(2,1)S(1)}, f32[128,1]{1,0:T(8,128)S(1)}, bf16[2,128,768]{2,1,0:T(8,128)(2,1)}) custom-call(s32[1]{0:T(128)} %bitcast.meta._, bf16[2,128,1024]{2,1,0:T(8,128)(2,1)} %get-tuple-element.32.mine, bf16[2,128,1024]{2,1,0:T(8,128)(2,1)} %collective-permute-done.4.other, bf16[1024,2048]{1,0:T(8,128)(2,1)} %q.13, ...), custom_call_target="tpu_custom_call" | custom-call | tf_op jit(solution)/shard_map/project_send/pallas_call | solution.py:213
  81.7 3.4 %project_keep.3.k1 = f32[2,128,768]{2,1,0:T(8,128)S(1)} custom-call(s32[1]{0:T(128)} %bitcast.meta._, bf16[2,128,1024]{2,1,0:T(8,128)(2,1)S(1)} %get-tuple-element.35.merged, bf16[1024,2048]{1,0:T(8,128)(2,1)} %q.13, bf16[1024,2048]{1,0:T(8,128)(2,1)} %collective-permute-done.5.qn, bf16[1024,1024]{1,0:T(8,128)(2,1)S(1)} %bitcast.33, ...), custom_call_target="tpu_custom_call" | custom-call | tf_op jit(solution)/shard_map/project_keep/pallas_call | solution.py:213
  85.1 3.6 %project_keep.2.k0 = f32[2,128,768]{2,1,0:T(8,128)S(1)} custom-call(s32[1]{0:T(128)} %bitcast.meta._, bf16[2,128,1024]{2,1,0:T(8,128)(2,1)S(1)} %get-tuple-element.33.merged, bf16[1024,2048]{1,0:T(8,128)(2,1)} %q.13, bf16[1024,2048]{1,0:T(8,128)(2,1)} %collective-permute-done.5.qn, bf16[1024,1024]{1,0:T(8,128)(2,1)S(1)} %bitcast.35, ...), custom_call_target="tpu_custom_call" | custom-call | tf_op jit(solution)/shard_map/project_keep/pallas_call | solution.py:213
  88.7 2.3 %collective-permute-done.11 = f32[2,128,1]{2,1,0:T(8,128)} collective-permute-done((f32[2,128,1]{2,1,0:T(8,128)}, f32[2,128,1]{2,1,0:T(8,128)}, u32[]{:S(2)}, u32[]{:S(2)}) %collective-permute-start.11) | collective-permute-done | bytes 1056 | tf_op jit(solution)/shard_map/ppermute | solution.py:185
  92.0 2.1 %scale_heads.1 = (bf16[2,128,768]{2,1,0:T(8,128)(2,1)S(1)}, bf16[2,128,768]{2,1,0:T(8,128)(2,1)}) custom-call(s32[1]{0:T(128)} %bitcast.meta._, f32[2,128,768]{2,1,0:T(8,128)S(1)} %project_keep.2.k0, f32[2,128,768]{2,1,0:T(8,128)S(1)} %project_keep.3.k1, bf16[2,128,768]{2,1,0:T(8,128)(2,1)} %collective-permute-done.9.g0, ...), custom_call_target="tpu_custom_call" | custom-call | tf_op jit(solution)/shard_map/scale_heads/pallas_call | solution.py:213
  100.8 5.5 %attention.1 = (bf16[128,768]{1,0:T(8,128)(2,1)S(1)}, bf16[128,768]{1,0:T(8,128)(2,1)S(1)}, bf16[2,128,768]{2,1,0:T(8,128)(2,1)S(1)}) custom-call(s32[1]{0:T(128)} %bitcast.meta._, bf16[2,128,768]{2,1,0:T(8,128)(2,1)S(1)} %copy-done.12, bf16[2,128,768]{2,1,0:T(8,128)(2,1)} %collective-permute-done.12.side, bf16[2,128,512]{2,1,0:T(8,128)(2,1)S(1)} %pad_maximum_fusion.g_mine, ...), custom_call_target="tpu_custom_call" | custom-call | tf_op jit(solution)/shard_map/attention/pallas_call | solution.py:213
  110.7 4.4 %dnormed_mine.1.acc = f32[256,2048]{1,0:T(8,128)S(1)} custom-call(s32[1]{0:T(128)} %bitcast.meta._, bf16[128,768]{1,0:T(8,128)(2,1)S(1)} %get-tuple-element.43.own, bf16[128,768]{1,0:T(8,128)(2,1)S(1)} %get-tuple-element.44.other, bf16[2,128,768]{2,1,0:T(8,128)(2,1)S(1)} %collective-permute-done.15.side, bf16[1024,2048]{1,0:T(8,128)(2,1)} %q.13, ...), custom_call_target="tpu_custom_call" | custom-call | tf_op jit(solution)/shard_map/dnormed_mine/pallas_call | solution.py:213
  115.1 7.6 %collective-permute-done.20.got_side = bf16[128,768]{1,0:T(8,128)(2,1)S(1)} collective-permute-done((bf16[128,768]{1,0:T(8,128)(2,1)S(1)}, bf16[128,768]{1,0:T(8,128)(2,1)S(1)}, u32[]{:S(2)}, u32[]{:S(2)}) %collective-permute-start.20) | collective-permute-done | bytes 196640 | tf_op jit(solution)/shard_map/ppermute | solution.py:185
  122.7 4.2 %dnormed_rest.3 = (bf16[2,128,1024]{2,1,0:T(8,128)(2,1)S(1)}, f32[128,1]{1,0:T(8,128)S(1)}) custom-call(s32[1]{0:T(128)} %bitcast.meta._, f32[256,2048]{1,0:T(8,128)S(1)} %dnormed_mine.1.acc, bf16[128,768]{1,0:T(8,128)(2,1)S(1)} %collective-permute-done.19.got, bf16[128,768]{1,0:T(8,128)(2,1)S(1)} %collective-permute-done.20.got_side, ...), custom_call_target="tpu_custom_call" | custom-call | tf_op jit(solution)/shard_map/dnormed_rest/pallas_call | solution.py:213
  126.9 4.4 %dnormed_rest.2 = (bf16[2,128,1024]{2,1,0:T(8,128)(2,1)S(1)}, f32[128,1]{1,0:T(8,128)S(1)}) custom-call(s32[1]{0:T(128)} %bitcast.meta._, f32[256,2048]{1,0:T(8,128)S(1)} %dnormed_mine.1.acc, bf16[128,768]{1,0:T(8,128)(2,1)S(1)} %collective-permute-done.16.got, bf16[128,768]{1,0:T(8,128)(2,1)S(1)} %collective-permute-done.17.got_side, ...), custom_call_target="tpu_custom_call" | custom-call | tf_op jit(solution)/shard_map/dnormed_rest/pallas_call | solution.py:213
  133.4 4.3 %collective-permute-done.21 = f32[2,128,1]{2,1,0:T(8,128)S(1)} collective-permute-done((f32[2,128,1]{2,1,0:T(8,128)S(1)}, f32[2,128,1]{2,1,0:T(8,128)S(1)}, u32[]{:S(2)}, u32[]{:S(2)}) %collective-permute-start.21) | collective-permute-done | bytes 1056 | tf_op jit(solution)/shard_map/ppermute | solution.py:189
  142.9 6.1 %collective-permute-done.23.other = bf16[2,128,1024]{2,1,0:T(8,128)(2,1)S(1)} collective-permute-done((bf16[2,128,1024]{2,1,0:T(8,128)(2,1)S(1)}, bf16[2,128,1024]{2,1,0:T(8,128)(2,1)S(1)}, u32[]{:S(2)}, u32[]{:S(2)}) %collective-permute-start.23) | collective-permute-done | bytes 524320 | tf_op jit(solution)/shard_map/ppermute | solution.py:189
  149.0 5.0 %dhidden.2 = bf16[128,1280]{1,0:T(8,128)(2,1)S(1)} custom-call(s32[1]{0:T(128)} %bitcast.meta._, bf16[2,128,1024]{2,1,0:T(8,128)(2,1)S(1)} %get-tuple-element.49.part, bf16[2,128,1024]{2,1,0:T(8,128)(2,1)S(1)} %collective-permute-done.23.other, bf16[2,128,1024]{2,1,0:T(8,128)(2,1)S(1)} %get-tuple-element.35.merged, f32[128,1]{1,0:T(8,128)S(1)} %get-tuple-element.61.rms, ...), custom_call_target="tpu_custom_call" | custom-call | tf_op jit(solution)/shard_map/dhidden/pallas_call | solution.py:213
  155.9 2.3 %collective-permute-done.18.other = bf16[2,128,1024]{2,1,0:T(8,128)(2,1)S(1)} collective-permute-done((bf16[2,128,1024]{2,1,0:T(8,128)(2,1)S(1)}, bf16[2,128,1024]{2,1,0:T(8,128)(2,1)S(1)}, u32[]{:S(2)}, u32[]{:S(2)}) %collective-permute-start.18) | collective-permute-done | bytes 524320 | tf_op jit(solution)/shard_map/ppermute | solution.py:189
  158.2 3.0 %collective-permute-done.24.rest_0_ = bf16[128,1280]{1,0:T(8,128)(2,1)S(1)} collective-permute-done((bf16[128,1280]{1,0:T(8,128)(2,1)S(1)}, bf16[128,1280]{1,0:T(8,128)(2,1)S(1)}, u32[]{:S(2)}, u32[]{:S(2)}) %collective-permute-start.24) | collective-permute-done | bytes 327712 | tf_op jit(solution)/shard_map/ppermute | solution.py:185
  161.2 5.1 %dhidden.3.own = bf16[128,1280]{1,0:T(8,128)(2,1)S(1)} custom-call(s32[1]{0:T(128)} %bitcast.meta._, bf16[2,128,1024]{2,1,0:T(8,128)(2,1)S(1)} %get-tuple-element.46.part, bf16[2,128,1024]{2,1,0:T(8,128)(2,1)S(1)} %collective-permute-done.18.other, bf16[2,128,1024]{2,1,0:T(8,128)(2,1)S(1)} %get-tuple-element.33.merged, f32[128,1]{1,0:T(8,128)S(1)} %get-tuple-element.62.rms, ...), custom_call_target="tpu_custom_call" | custom-call | tf_op jit(solution)/shard_map/dhidden/pallas_call | solution.py:213
  168.1 5.3 %collective-permute-done.25.other = bf16[128,1280]{1,0:T(8,128)(2,1)S(1)} collective-permute-done((bf16[128,1280]{1,0:T(8,128)(2,1)S(1)}, bf16[128,1280]{1,0:T(8,128)(2,1)S(1)}, u32[]{:S(2)}, u32[]{:S(2)}) %collective-permute-start.25) | collective-permute-done | bytes 327712 | tf_op jit(solution)/shard_map/ppermute | solution.py:185
  173.5 4.5 %dmerge.1 = (bf16[2,128,640]{2,1,0:T(8,128)(2,1)S(1)}, bf16[2,128,640]{2,1,0:T(8,128)(2,1)S(1)}) custom-call(s32[1]{0:T(128)} %bitcast.meta._, bf16[128,1280]{1,0:T(8,128)(2,1)S(1)} %dhidden.3.own, bf16[128,1280]{1,0:T(8,128)(2,1)S(1)} %collective-permute-done.25.other, bf16[640,1280]{1,0:T(8,128)(2,1)S(1)} %bitcast.46, ...), custom_call_target="tpu_custom_call" | custom-call | tf_op jit(solution)/shard_map/dmerge/pallas_call | solution.py:213
  179.8 5.3 %collective-permute-done.26.got = bf16[2,128,640]{2,1,0:T(8,128)(2,1)S(1)} collective-permute-done((bf16[2,128,640]{2,1,0:T(8,128)(2,1)S(1)}, bf16[2,128,640]{2,1,0:T(8,128)(2,1)S(1)}, u32[]{:S(2)}, u32[]{:S(2)}) %collective-permute-start.26) | collective-permute-done | bytes 327712 | tf_op jit(solution)/shard_map/ppermute | solution.py:189
  187.0 3.6 %collective-permute-done.27.other = bf16[2,64,640]{2,1,0:T(8,128)(2,1)S(1)} collective-permute-done((bf16[2,64,640]{2,1,0:T(8,128)(2,1)S(1)}, bf16[2,64,640]{2,1,0:T(8,128)(2,1)S(1)}, u32[]{:S(2)}, u32[]{:S(2)}) %collective-permute-start.27) | collective-permute-done | bytes 163872 | tf_op jit(solution)/shard_map/ppermute | solution.py:185
  (92 shorter events, 49.8 us)
Async XLA Ops:
  0.0 60.8 %collective-permute-start.5 = (bf16[1024,2048]{1,0:T(8,128)(2,1)}, bf16[1024,2048]{1,0:T(8,128)(2,1)}, u32[]{:S(2)}, u32[]{:S(2)}) collective-permute-start(bf16[1024,2048]{1,0:T(8,128)(2,1)} %q.13), channel_id=1, source_target_pairs={{0,2},{2,0},{4,6},{6,4},{1,3},{3,1},{5,7},{7,5},{8,10},{10,8},{12,... | collective-permute-start | bytes 12582920 | tf_op jit(solution)/shard_map/ppermute | solution.py:180
  0.5 27.9 %collective-permute-start.3 = (bf16[1280,1024]{1,0:T(8,128)(2,1)}, bf16[1280,1024]{1,0:T(8,128)(2,1)}, u32[]{:S(2)}, u32[]{:S(2)}) collective-permute-start(bf16[1280,1024]{1,0:T(8,128)(2,1)} %w.7), channel_id=1, source_target_pairs={{0,2},{2,0},{4,6},{6,4},{1,3},{3,1},{5,7},{7,5},{8,10},{10,8},{12,... | collective-permute-start | bytes 7864328 | tf_op jit(solution)/shard_map/ppermute | solution.py:180
  0.5 14.8 %collective-permute-start = (bf16[640,1280]{1,0:T(8,128)(2,1)}, bf16[640,1280]{1,0:T(8,128)(2,1)}, u32[]{:S(2)}, u32[]{:S(2)}) collective-permute-start(bf16[640,1280]{1,0:T(8,128)(2,1)} %bitcast.43), channel_id=1, source_target_pairs={{0,2},{2,0},{4,6},{6,4},{1,3},{3,1},{5,7},{7,5},{8,10},{10,8},{12,... | collective-permute-start | bytes 4915208 | tf_op jit(solution)/shard_map/ppermute | solution.py:180
  3.2 46.0 %collective-permute-start.6 = (bf16[1024,1024]{1,0:T(8,128)(2,1)S(1)}, bf16[1024,1024]{1,0:T(8,128)(2,1)}, u32[]{:S(2)}, u32[]{:S(2)}) collective-permute-start(bf16[1024,1024]{1,0:T(8,128)(2,1)S(1)} %bitcast.28), channel_id=1, source_target_pairs={{0,2},{2,0},{4,6},{6,4},{1,3},{3,1},{5,7},{7,5},{8,10},{10,8},{12,... | collective-permute-start | bytes 6291464 | tf_op jit(solution)/shard_map/ppermute | solution.py:180
  4.3 11.0 %collective-permute-start.1 = (bf16[2,128,640]{2,1,0:T(8,128)(2,1)S(1)}, bf16[2,128,640]{2,1,0:T(8,128)(2,1)S(1)}, u32[]{:S(2)}, u32[]{:S(2)}) collective-permute-start(bf16[2,128,640]{2,1,0:T(8,128)(2,1)S(1)} %get-tuple-element.30), channel_id=1, source_target_pairs={{0,4},{2,6},{4,0},{6,2},{1,5},{3,7},{5,1},{7,3},{8,12},{10,14},{12... | collective-permute-start | bytes 983048 | tf_op jit(solution)/shard_map/ppermute | solution.py:185
  19.0 9.4 %collective-permute-start.2 = (bf16[128,1280]{1,0:T(8,128)(2,1)S(1)}, bf16[128,1280]{1,0:T(8,128)(2,1)S(1)}, u32[]{:S(2)}, u32[]{:S(2)}) collective-permute-start(bf16[128,1280]{1,0:T(8,128)(2,1)S(1)} %first.3), channel_id=1, source_target_pairs={{0,4},{2,6},{4,0},{6,2},{1,5},{3,7},{5,1},{7,3},{8,12},{10,14},{12... | collective-permute-start | bytes 983048 | tf_op jit(solution)/shard_map/ppermute | solution.py:185
  33.1 8.5 %collective-permute-start.7 = (bf16[128,1280]{1,0:T(8,128)(2,1)S(1)}, bf16[128,1280]{1,0:T(8,128)(2,1)S(1)}, u32[]{:S(2)}, u32[]{:S(2)}) collective-permute-start(bf16[128,1280]{1,0:T(8,128)(2,1)S(1)} %get-tuple-element.34), channel_id=1, source_target_pairs={{0,4},{2,6},{4,0},{6,2},{1,5},{3,7},{5,1},{7,3},{8,12},{10,14},{12... | collective-permute-start | bytes 983048 | tf_op jit(solution)/shard_map/ppermute | solution.py:185
  45.1 14.9 %collective-permute-start.8 = (bf16[2,128,1024]{2,1,0:T(8,128)(2,1)S(1)}, bf16[2,128,1024]{2,1,0:T(8,128)(2,1)S(1)}, u32[]{:S(2)}, u32[]{:S(2)}) collective-permute-start(bf16[2,128,1024]{2,1,0:T(8,128)(2,1)S(1)} %merge_far.1.mine), channel_id=1, source_target_pairs={{0,1},{1,0},{2,3},{3,2},{4,5},{5,4},{6,7},{7,6},{8,9},{9,8},{10,11... | collective-permute-start | bytes 1572872 | tf_op jit(solution)/shard_map/ppermute | solution.py:189
  46.9 21.4 %collective-permute-start.4 = (bf16[2,128,1024]{2,1,0:T(8,128)(2,1)}, bf16[2,128,1024]{2,1,0:T(8,128)(2,1)}, u32[]{:S(2)}, u32[]{:S(2)}) collective-permute-start(bf16[2,128,1024]{2,1,0:T(8,128)(2,1)} %get-tuple-element.32.mine), channel_id=1, source_target_pairs={{0,1},{1,0},{2,3},{3,2},{4,5},{5,4},{6,7},{7,6},{8,9},{9,8},{10,11... | collective-permute-start | bytes 1572872 | tf_op jit(solution)/shard_map/ppermute | solution.py:189
  66.0 25.9 %collective-permute-start.9 = (bf16[2,128,768]{2,1,0:T(8,128)(2,1)}, bf16[2,128,768]{2,1,0:T(8,128)(2,1)}, u32[]{:S(2)}, u32[]{:S(2)}) collective-permute-start(bf16[2,128,768]{2,1,0:T(8,128)(2,1)} %get-tuple-element.36), channel_id=1, source_target_pairs={{0,4},{2,6},{4,0},{6,2},{1,5},{3,7},{5,1},{7,3},{8,12},{10,14},{12... | collective-permute-start | bytes 1179656 | tf_op jit(solution)/shard_map/ppermute | solution.py:185
  72.9 19.0 %collective-permute-start.10 = (bf16[2,128,768]{2,1,0:T(8,128)(2,1)}, bf16[2,128,768]{2,1,0:T(8,128)(2,1)}, u32[]{:S(2)}, u32[]{:S(2)}) collective-permute-start(bf16[2,128,768]{2,1,0:T(8,128)(2,1)} %get-tuple-element.37), channel_id=1, source_target_pairs={{0,4},{2,6},{4,0},{6,2},{1,5},{3,7},{5,1},{7,3},{8,12},{10,14},{12... | collective-permute-start | bytes 1179656 | tf_op jit(solution)/shard_map/ppermute | solution.py:185
  77.2 16.8 %collective-permute-start.13 = (bf16[2,128,512]{2,1,0:T(8,128)(2,1)}, bf16[2,128,512]{2,1,0:T(8,128)(2,1)}, u32[]{:S(2)}, u32[]{:S(2)}) collective-permute-start(bf16[2,128,512]{2,1,0:T(8,128)(2,1)} %bitcast.64), channel_id=1, source_target_pairs={{0,4},{2,6},{4,0},{6,2},{1,5},{3,7},{5,1},{7,3},{8,12},{10,14},{12... | collective-permute-start | bytes 786440 | tf_op jit(solution)/shard_map/ppermute | solution.py:185
  78.2 12.8 %collective-permute-start.11 = (f32[2,128,1]{2,1,0:T(8,128)}, f32[2,128,1]{2,1,0:T(8,128)}, u32[]{:S(2)}, u32[]{:S(2)}) collective-permute-start(f32[2,128,1]{2,1,0:T(8,128)} %pad_maximum_fusion.2), channel_id=1, source_target_pairs={{0,4},{2,6},{4,0},{6,2},{1,5},{3,7},{5,1},{7,3},{8,12},{10,14},{12... | collective-permute-start | bytes 3080 | tf_op jit(solution)/shard_map/ppermute | solution.py:185
  94.0 5.7 %collective-permute-start.12 = (bf16[2,128,768]{2,1,0:T(8,128)(2,1)}, bf16[2,128,768]{2,1,0:T(8,128)(2,1)}, u32[]{:S(2)}, u32[]{:S(2)}) collective-permute-start(bf16[2,128,768]{2,1,0:T(8,128)(2,1)} %get-tuple-element.41), channel_id=1, source_target_pairs={{0,2},{2,0},{4,6},{6,4},{1,3},{3,1},{5,7},{7,5},{8,10},{10,8},{12,... | collective-permute-start | bytes 1179656 | tf_op jit(solution)/shard_map/ppermute | solution.py:180
  96.6 3.2 %collective-permute-start.14 = (bf16[2,128,512]{2,1,0:T(8,128)(2,1)}, bf16[2,128,512]{2,1,0:T(8,128)(2,1)}, u32[]{:S(2)}, u32[]{:S(2)}) collective-permute-start(bf16[2,128,512]{2,1,0:T(8,128)(2,1)} %pad_maximum_fusion.1), channel_id=1, source_target_pairs={{0,2},{2,0},{4,6},{6,4},{1,3},{3,1},{5,7},{7,5},{8,10},{10,8},{12,... | collective-permute-start | bytes 786440 | tf_op jit(solution)/shard_map/ppermute | solution.py:180
  106.3 2.2 %collective-permute-start.15 = (bf16[2,128,768]{2,1,0:T(8,128)(2,1)S(1)}, bf16[2,128,768]{2,1,0:T(8,128)(2,1)S(1)}, u32[]{:S(2)}, u32[]{:S(2)}) collective-permute-start(bf16[2,128,768]{2,1,0:T(8,128)(2,1)S(1)} %get-tuple-element.45), channel_id=1, source_target_pairs={{0,2},{2,0},{4,6},{6,4},{1,3},{3,1},{5,7},{7,5},{8,10},{10,8},{12,... | collective-permute-start | bytes 1179656 | tf_op jit(solution)/shard_map/ppermute | solution.py:180
  106.5 8.6 %collective-permute-start.19 = (bf16[128,768]{1,0:T(8,128)(2,1)S(1)}, bf16[128,768]{1,0:T(8,128)(2,1)S(1)}, u32[]{:S(2)}, u32[]{:S(2)}) collective-permute-start(bf16[128,768]{1,0:T(8,128)(2,1)S(1)} %get-tuple-element.43.own), channel_id=1, source_target_pairs={{0,4},{2,6},{4,0},{6,2},{1,5},{3,7},{5,1},{7,3},{8,12},{10,14},{12... | collective-permute-start | bytes 589832 | tf_op jit(solution)/shard_map/ppermute | solution.py:185
  108.2 18.7 %collective-permute-start.16 = (bf16[128,768]{1,0:T(8,128)(2,1)S(1)}, bf16[128,768]{1,0:T(8,128)(2,1)S(1)}, u32[]{:S(2)}, u32[]{:S(2)}) collective-permute-start(bf16[128,768]{1,0:T(8,128)(2,1)S(1)} %get-tuple-element.44.other), channel_id=1, source_target_pairs={{0,4},{2,6},{4,0},{6,2},{1,5},{3,7},{5,1},{7,3},{8,12},{10,14},{12... | collective-permute-start | bytes 589832 | tf_op jit(solution)/shard_map/ppermute | solution.py:185
  108.6 14.1 %collective-permute-start.20 = (bf16[128,768]{1,0:T(8,128)(2,1)S(1)}, bf16[128,768]{1,0:T(8,128)(2,1)S(1)}, u32[]{:S(2)}, u32[]{:S(2)}) collective-permute-start(bf16[128,768]{1,0:T(8,128)(2,1)S(1)} %get-tuple-element.55), channel_id=1, source_target_pairs={{0,4},{2,6},{4,0},{6,2},{1,5},{3,7},{5,1},{7,3},{8,12},{10,14},{12... | collective-permute-start | bytes 589832 | tf_op jit(solution)/shard_map/ppermute | solution.py:185
  110.4 16.6 %collective-permute-start.17 = (bf16[128,768]{1,0:T(8,128)(2,1)S(1)}, bf16[128,768]{1,0:T(8,128)(2,1)S(1)}, u32[]{:S(2)}, u32[]{:S(2)}) collective-permute-start(bf16[128,768]{1,0:T(8,128)(2,1)S(1)} %get-tuple-element.56), channel_id=1, source_target_pairs={{0,4},{2,6},{4,0},{6,2},{1,5},{3,7},{5,1},{7,3},{8,12},{10,14},{12... | collective-permute-start | bytes 589832 | tf_op jit(solution)/shard_map/ppermute | solution.py:185
  126.9 22.1 %copy-start.1 = (bf16[1280,1024]{1,0:T(8,128)(2,1)S(1)}, bf16[1280,1024]{1,0:T(8,128)(2,1)}, u32[]{:S(2)}) copy-start(bf16[1280,1024]{1,0:T(8,128)(2,1)} %w.7) | copy-start | bytes 7864324
  131.3 6.4 %collective-permute-start.21 = (f32[2,128,1]{2,1,0:T(8,128)S(1)}, f32[2,128,1]{2,1,0:T(8,128)S(1)}, u32[]{:S(2)}, u32[]{:S(2)}) collective-permute-start(f32[2,128,1]{2,1,0:T(8,128)S(1)} %pad_maximum_fusion.3), channel_id=1, source_target_pairs={{0,1},{1,0},{2,3},{3,2},{4,5},{5,4},{6,7},{7,6},{8,9},{9,8},{10,11... | collective-permute-start | bytes 3080 | tf_op jit(solution)/shard_map/ppermute | solution.py:189
  133.1 15.9 %collective-permute-start.23 = (bf16[2,128,1024]{2,1,0:T(8,128)(2,1)S(1)}, bf16[2,128,1024]{2,1,0:T(8,128)(2,1)S(1)}, u32[]{:S(2)}, u32[]{:S(2)}) collective-permute-start(bf16[2,128,1024]{2,1,0:T(8,128)(2,1)S(1)} %get-tuple-element.49.part), channel_id=1, source_target_pairs={{0,1},{1,0},{2,3},{3,2},{4,5},{5,4},{6,7},{7,6},{8,9},{9,8},{10,11... | collective-permute-start | bytes 1572872 | tf_op jit(solution)/shard_map/ppermute | solution.py:189
  137.8 5.0 %collective-permute-start.22 = (f32[2,128,1]{2,1,0:T(8,128)S(1)}, f32[2,128,1]{2,1,0:T(8,128)S(1)}, u32[]{:S(2)}, u32[]{:S(2)}) collective-permute-start(f32[2,128,1]{2,1,0:T(8,128)S(1)} %fusion), channel_id=1, source_target_pairs={{0,4},{2,6},{4,0},{6,2},{1,5},{3,7},{5,1},{7,3},{8,12},{10,14},{12... | collective-permute-start | bytes 3080 | tf_op jit(solution)/shard_map/ppermute | solution.py:185
  139.6 18.6 %collective-permute-start.18 = (bf16[2,128,1024]{2,1,0:T(8,128)(2,1)S(1)}, bf16[2,128,1024]{2,1,0:T(8,128)(2,1)S(1)}, u32[]{:S(2)}, u32[]{:S(2)}) collective-permute-start(bf16[2,128,1024]{2,1,0:T(8,128)(2,1)S(1)} %get-tuple-element.46.part), channel_id=1, source_target_pairs={{0,1},{1,0},{2,3},{3,2},{4,5},{5,4},{6,7},{7,6},{8,9},{9,8},{10,11... | collective-permute-start | bytes 1572872 | tf_op jit(solution)/shard_map/ppermute | solution.py:189
  149.0 12.2 %copy-start.8 = (f32[128,1280]{1,0:T(8,128)S(1)}, f32[128,1280]{1,0:T(8,128)}, u32[]{:S(2)}) copy-start(f32[128,1280]{1,0:T(8,128)} %copy-done.7) | copy-start | bytes 1966084
  154.1 7.1 %collective-permute-start.24 = (bf16[128,1280]{1,0:T(8,128)(2,1)S(1)}, bf16[128,1280]{1,0:T(8,128)(2,1)S(1)}, u32[]{:S(2)}, u32[]{:S(2)}) collective-permute-start(bf16[128,1280]{1,0:T(8,128)(2,1)S(1)} %dhidden.2), channel_id=1, source_target_pairs={{0,4},{2,6},{4,0},{6,2},{1,5},{3,7},{5,1},{7,3},{8,12},{10,14},{12... | collective-permute-start | bytes 983048 | tf_op jit(solution)/shard_map/ppermute | solution.py:185
  161.2 12.3 %copy-start.4 = (bf16[4,160,1280]{2,1,0:T(8,128)(2,1)S(1)}, bf16[4,160,1280]{2,1,0:T(8,128)(2,1)}, u32[]{:S(2)}) copy-start(bf16[4,160,1280]{2,1,0:T(8,128)(2,1)} %param.8) | copy-start | bytes 4915204
  166.3 24.2 %copy-start.6 = (bf16[512,640]{1,0:T(8,128)(2,1)S(1)}, bf16[512,640]{1,0:T(8,128)(2,1)}, u32[]{:S(2)}) copy-start(bf16[512,640]{1,0:T(8,128)(2,1)} %x.3) | copy-start | bytes 1966084
  166.3 7.1 %collective-permute-start.25 = (bf16[128,1280]{1,0:T(8,128)(2,1)S(1)}, bf16[128,1280]{1,0:T(8,128)(2,1)S(1)}, u32[]{:S(2)}, u32[]{:S(2)}) collective-permute-start(bf16[128,1280]{1,0:T(8,128)(2,1)S(1)} %dhidden.3.own), channel_id=1, source_target_pairs={{0,4},{2,6},{4,0},{6,2},{1,5},{3,7},{5,1},{7,3},{8,12},{10,14},{12... | collective-permute-start | bytes 983048 | tf_op jit(solution)/shard_map/ppermute | solution.py:185
  178.0 7.1 %collective-permute-start.26 = (bf16[2,128,640]{2,1,0:T(8,128)(2,1)S(1)}, bf16[2,128,640]{2,1,0:T(8,128)(2,1)S(1)}, u32[]{:S(2)}, u32[]{:S(2)}) collective-permute-start(bf16[2,128,640]{2,1,0:T(8,128)(2,1)S(1)} %get-tuple-element.52), channel_id=1, source_target_pairs={{0,1},{1,0},{2,3},{3,2},{4,5},{5,4},{6,7},{7,6},{8,9},{9,8},{10,11... | collective-permute-start | bytes 983048 | tf_op jit(solution)/shard_map/ppermute | solution.py:189
  185.2 5.4 %collective-permute-start.27 = (bf16[2,64,640]{2,1,0:T(8,128)(2,1)S(1)}, bf16[2,64,640]{2,1,0:T(8,128)(2,1)S(1)}, u32[]{:S(2)}, u32[]{:S(2)}) collective-permute-start(bf16[2,64,640]{2,1,0:T(8,128)(2,1)S(1)} %add_convert_fusion), channel_id=1, source_target_pairs={{0,4},{2,6},{4,0},{6,2},{1,5},{3,7},{5,1},{7,3},{8,12},{10,14},{12... | collective-permute-start | bytes 491528 | tf_op jit(solution)/shard_map/ppermute | solution.py:185
  (11 other events, 50.1 us)
